TPU v7x, 32 devices: a whole 2x2x4 slice. The times are simulated.
32 devices in a mesh: nodes: 8 (over z, x), heads: 4 (over y, core).
Axes of the slice: x: 2, y: 2, z: 4, core: 2. Of those that a mesh axis runs over, the one named last changes fastest.
Arguments:
- nodes_in: bfloat16 [4096, 1024], P('nodes', 'heads'), may hold values from -6 to 6
- local_gain: float32 [1024], replicated, may hold values from 0.5 to 1.5
- neighbour_query_key_value: bfloat16 [3, 1024, 1024], P(None, None, 'heads'), may hold values from -0.25 to 0.25
- local_out: bfloat16 [1024, 1024], P('heads'), may hold values from -0.1875 to 0.1875
- global_gain: float32 [1024], replicated, may hold values from 0.5 to 1.5
- global_qkv: bfloat16 [3, 1024, 1024], P(None, None, 'heads'), may hold values from -0.1875 to 0.1875
- global_out: bfloat16 [1024, 1024], P('heads'), may hold values from -1.875 to 1.875
- feature_map: bfloat16 [16, 64, 128], P('heads'), may hold values from -5 to 5
- neighbour_count: int32 [32], P('nodes'), may hold values from 1 to 8
- neighbour_blocks: int32 [32, 8], P('nodes'), may hold values from 0 to 31, as said below
- metis_order: int32 [32], P('nodes'), may hold values from 0 to 31, as said below
- hashed_order: int32 [32], P('nodes'), may hold values from 0 to 31, as said below
Outputs:
- output: bfloat16 [4096, 1024], P('nodes', 'heads')
Inputs may be any that keep to these rules, and one draw needn't show every extreme that they name: `neighbour_blocks`: entry 0 of block b's list is b itself; every entry lies within 2 blocks of the aligned group of 4 blocks that holds b, inside the graph; entries from neighbour_count on are unused; entries may repeat. `metis_order`: A permutation of the block ids. `hashed_order`: A permutation of the block ids. The blocks at the 4 METIS positions of aligned group g go to the aligned groups of 4 hashed positions numbered (g + k * 2) modulo 8 for k = 0 to 3, exactly 1 of them to each; which block goes to which of these groups, and to which position in it, is drawn.
All inputs are finite; a program needn't handle non-finite values.
Results may differ from a plain program's by a relative error of at most 0.015.
Values may be sent and summed in bfloat16 or wider, within the bound.
A program may use at most 64 MiB of HBM per device.

v0:
```python
import jax
import jax.numpy as jnp
from jax import lax
from jax.sharding import PartitionSpec as P

HD = 64
BLOCK = 128
HALO_BLK = 2


EPSILON = 1e-06


def passed_along(value, axis, steps):
    count = lax.axis_size(axis)
    pairs = [(source, (source + steps) % count) for source in range(count)]
    return lax.ppermute(value, axis, pairs)


def padded(array, sides, width):
    for axis, dim in sides:
        count, length = (lax.axis_size(axis), array.shape[dim])
        up = [(i, (i + 1) % count) for i in range(count - 1)]
        down = [(j, i) for i, j in up]
        last = lax.slice_in_dim(array, length - width, length, axis=dim)
        initial = lax.slice_in_dim(array, 0, width, axis=dim)
        before = lax.ppermute(last, axis, up)
        after = lax.ppermute(initial, axis, down)
        array = jnp.concatenate([before, array, after], axis=dim)
    return array


def root_scale(row_data, gain_vector):
    as_float = row_data.astype(jnp.float32)
    mean_square = jnp.mean(as_float * as_float, axis=-1, keepdims=True)
    return (as_float * lax.rsqrt(mean_square + EPSILON) * gain_vector).astype(jnp.bfloat16)


def local_attention(queries, extended, counts, local_index):
    block_count = counts.shape[0]
    list_slots = local_index.shape[1]
    group_size = 4
    feature_width = queries.shape[1]
    heads_local = feature_width // HD
    key_blocks = extended.reshape(2, -1, BLOCK, feature_width)
    query_groups = queries.reshape(block_count // group_size, group_size, BLOCK, heads_local, HD)
    slot_of_key = jnp.arange(list_slots * BLOCK, dtype=jnp.int32) // BLOCK

    def one_group(inputs):
        query_group, index_group, count_group = inputs
        picked = key_blocks[:, index_group].reshape(
            2, group_size, list_slots * BLOCK, heads_local, HD
        )
        scores = jnp.einsum(
            "gqhd,gkhd->ghqk", query_group, picked[0], preferred_element_type=jnp.float32
        ) * HD ** (-0.5)
        live = slot_of_key[None, :] < count_group[:, None]
        scores = jnp.where(live[:, None, None, :], scores, -jnp.inf)
        row_max = jnp.max(scores, axis=-1, keepdims=True)
        expo = jnp.exp(scores - row_max)
        totals = jnp.sum(expo, axis=-1)
        local_weights = expo.astype(jnp.bfloat16)
        mixed_heads = jnp.einsum(
            "ghqk,gkhd->gqhd", local_weights, picked[1], preferred_element_type=jnp.float32
        )
        mixed_heads = mixed_heads / jnp.transpose(totals, (0, 2, 1))[..., None]
        return mixed_heads.astype(jnp.bfloat16)

    mixed_all = lax.map(
        one_group,
        (
            query_groups,
            local_index.reshape(block_count // group_size, group_size, list_slots),
            counts.reshape(block_count // group_size, group_size),
        ),
    )
    return mixed_all.reshape(block_count * BLOCK, feature_width)


def relayout(row_data, metis_local, all_hashed, device_nodes):
    block_count = metis_local.shape[0]
    devices = lax.axis_size("nodes")
    lane_count = min(block_count, devices)
    stride = max(1, devices // block_count)
    slot_limit = block_count // lane_count
    feature_width = row_data.shape[1]
    total_blocks = all_hashed.shape[0]
    matches = all_hashed[None, :] == metis_local[:, None]
    target = jnp.sum(
        jnp.where(matches, jnp.arange(total_blocks, dtype=jnp.int32)[None, :], 0), axis=1
    )
    steps_away = (target // block_count - device_nodes) % devices // stride
    order_ids = jnp.arange(block_count, dtype=jnp.int32)
    earlier = (steps_away[None, :] == steps_away[:, None]) & (
        order_ids[None, :] < order_ids[:, None]
    )
    rank_within = jnp.sum(earlier.astype(jnp.int32), axis=1)
    lane_id = rank_within * lane_count + steps_away
    chosen = lane_id[None, :] == order_ids[:, None]
    source = jnp.sum(jnp.where(chosen, order_ids[None, :], 0), axis=1)
    lane_target = jnp.sum(jnp.where(chosen, target[None, :], 0), axis=1)
    blocks = row_data.reshape(block_count, BLOCK, feature_width)
    outgoing = blocks[source].reshape(slot_limit, lane_count, BLOCK, feature_width)
    positions = lane_target.reshape(slot_limit, lane_count)
    block_pieces = [outgoing[:, :1]]
    position_pieces = [positions[:, :1]]
    for lane_step in range(1, lane_count):
        arrived, arrived_at = passed_along(
            (outgoing[:, lane_step : lane_step + 1], positions[:, lane_step : lane_step + 1]),
            "nodes",
            lane_step * stride,
        )
        block_pieces.append(arrived)
        position_pieces.append(arrived_at)
    incoming = jnp.concatenate(block_pieces, axis=1)
    in_position = jnp.concatenate(position_pieces, axis=1)
    local_position = in_position.reshape(block_count) - device_nodes * block_count
    located = local_position[None, :] == order_ids[:, None]
    picked_lane = jnp.sum(jnp.where(located, order_ids[None, :], 0), axis=1)
    return incoming.reshape(block_count, BLOCK, feature_width)[picked_lane].reshape(
        block_count * BLOCK, feature_width
    )


def feature_shard(full_rows, device_heads, feature_width):
    return lax.dynamic_slice_in_dim(full_rows, device_heads * feature_width, feature_width, 1)


def global_mixing(full_rows, gain_vector, triple_weight, feature_map, out_weight):
    rescaled_input = root_scale(full_rows, gain_vector)
    triple = jnp.einsum(
        "au,nuz->naz", rescaled_input, triple_weight, preferred_element_type=jnp.float32
    ).astype(jnp.bfloat16)
    row_count = full_rows.shape[0]
    heads_local = feature_map.shape[0]

    def feature_maps(head_rows):
        angles = jnp.einsum(
            "nhd,hdf->nhf",
            head_rows.reshape(row_count, heads_local, HD),
            feature_map,
            preferred_element_type=jnp.float32,
        ) * HD ** (-0.5)
        return (jax.nn.elu(angles) + 1.0).astype(jnp.bfloat16)

    phi_query = feature_maps(triple[0])
    phi_key = feature_maps(triple[1])
    head_values = triple[2].reshape(row_count, heads_local, HD)
    summary = jnp.einsum("nhf,nhd->hfd", phi_key, head_values, preferred_element_type=jnp.float32)
    key_total = jnp.sum(phi_key.astype(jnp.float32), axis=0)
    summary, key_total = lax.psum((summary, key_total), "nodes")
    query_float = phi_query.astype(jnp.float32)
    numerator = jnp.einsum("nhf,hfd->nhd", query_float, summary, precision=lax.Precision.HIGHEST)
    denominator = jnp.einsum("nhf,hf->nh", query_float, key_total, precision=lax.Precision.HIGHEST)
    global_mixed = (
        (numerator / denominator[..., None])
        .astype(jnp.bfloat16)
        .reshape(row_count, heads_local * HD)
    )
    return jnp.dot(global_mixed, out_weight, preferred_element_type=jnp.float32)


def body(
    nodes_in,
    local_gain,
    neighbour_query_key_value,
    local_out,
    global_gain,
    global_qkv,
    global_out,
    feature_map,
    neighbour_count,
    neighbour_blocks,
    metis_order,
    hashed_order,
):
    block_count = metis_order.shape[0]
    feature_width = nodes_in.shape[1]
    device_nodes = lax.axis_index("nodes")
    device_heads = lax.axis_index("heads")
    all_hashed = lax.all_gather(hashed_order, "nodes", axis=0, tiled=True)
    full_input = lax.all_gather(nodes_in, "heads", axis=1, tiled=True)
    local_rescaled = root_scale(full_input, local_gain)
    triple = jnp.einsum(
        "au,nuz->naz", local_rescaled, neighbour_query_key_value, preferred_element_type=jnp.float32
    ).astype(jnp.bfloat16)
    rim_rows = HALO_BLK * BLOCK
    extended = padded(triple[1:], (("nodes", 1),), rim_rows)
    first_block = device_nodes * block_count - HALO_BLK
    local_index = neighbour_blocks - first_block
    local_mixed = local_attention(triple[0], extended, neighbour_count, local_index)
    partial_value = jnp.dot(local_mixed, local_out, preferred_element_type=jnp.float32)
    summed = lax.psum(partial_value.astype(jnp.bfloat16), "heads").astype(jnp.float32)
    hidden = (full_input.astype(jnp.float32) + summed).astype(jnp.bfloat16)
    residual_part = feature_shard(hidden, device_heads, feature_width)
    global_partial = global_mixing(hidden, global_gain, global_qkv, feature_map, global_out)
    global_summed = lax.psum_scatter(
        global_partial.astype(jnp.bfloat16), "heads", scatter_dimension=1, tiled=True
    ).astype(jnp.float32)
    result = (residual_part.astype(jnp.float32) + global_summed).astype(jnp.bfloat16)
    result = relayout(result, metis_order, all_hashed, device_nodes)
    return result


def solution(mesh):
    in_specs = (
        P("nodes", "heads"),
        P(),
        P(None, None, "heads"),
        P("heads", None),
        P(),
        P(None, None, "heads"),
        P("heads", None),
        P("heads", None, None),
        P("nodes"),
        P("nodes", None),
        P("nodes"),
        P("nodes"),
    )
    out_specs = P("nodes", "heads")
    return jax.shard_map(body, mesh=mesh, in_specs=in_specs, out_specs=out_specs, check_vma=False)
```

profile of v0, /device:TPU:0, one launch (start us, length us, event | category | flops | bytes accessed | tf_op | source)
XLA Modules:
  0.0 240.6 jit_solution(2433115595511134121)
XLA Ops:
  6.5 0.7 all-gather.2.cloned.1.call-update
  7.3 0.7 compare_select_fusion.4
  8.1 20.4 %all-gather.2.cloned.1.call-done = bf16[512,1024]{1,0:T(8,128)(2,1)} async-done(((bf16[512,256]{1,0:T(8,128)(2,1)}), bf16[512,1024]{1,0:T(8,128)(2,1)}) %all-gather.2.cloned.1.call-update) | async-done | bytes 1048592 | tf_op jit(solution)/shard_map/all_gather | solution.py:182
  28.5 1.5 fusion.9
  30.0 2.3 fusion.15
  32.3 1.3 collective-permute-start.1
  33.6 5.3 %collective-permute-start = (bf16[2,256,256]{2,1,0:T(8,128)(2,1)S(1)}, bf16[2,256,256]{2,1,0:T(8,128)(2,1)}, u32[]{:S(2)}, u32[]{:S(2)}) collective-permute-start(bf16[2,256,256]{2,1,0:T(8,128)(2,1)S(1)} %get-tuple-element.35), channel_id=1, source_target_pairs={{0,4},{4,8},{8,12},{12,16},{16,20},{20,24},{24,28},{1,5},{5,9},{9,... | collective-permute-start | bytes 786440 | tf_op jit(solution)/shard_map/ppermute | solution.py:27
  39.0 0.8 slice.81
  40.0 2.6 %collective-permute-done.1 = bf16[2,256,256]{2,1,0:T(8,128)(2,1)S(1)} collective-permute-done((bf16[2,256,256]{2,1,0:T(8,128)(2,1)S(1)}, bf16[2,256,256]{2,1,0:T(8,128)(2,1)S(1)}, u32[]{:S(2)}, u32[]{:S(2)}) %collective-permute-start.1) | collective-permute-done | bytes 262176 | tf_op jit(solution)/shard_map/ppermute | solution.py:28
  42.7 5.5 %collective-permute-done = bf16[2,256,256]{2,1,0:T(8,128)(2,1)} collective-permute-done((bf16[2,256,256]{2,1,0:T(8,128)(2,1)S(1)}, bf16[2,256,256]{2,1,0:T(8,128)(2,1)}, u32[]{:S(2)}, u32[]{:S(2)}) %collective-permute-start) | collective-permute-done | bytes 262176 | tf_op jit(solution)/shard_map/ppermute | solution.py:27
  48.2 1.2 pad_maximum_fusion
  49.3 2.8 %gather_fusion = bf16[32,2,128,256]{3,2,1,0:T(8,128)(2,1)} fusion(bf16[2,8,128,256]{3,2,1,0:T(8,128)(2,1)S(1)} %bitcast.105, s32[1024]{0:T(1024)S(1)} %pad_clamp_fusion.2), kind=kCustom, calls=%fused_computation | custom fusion | bytes 8388736 | tf_op jit(solution)/shard_map/while/body/eval_jaxpr/gather | solution.py:51
  52.1 7.5 %copy.21 = bf16[4,8,2,128,256]{3,1,4,0,2:T(8,128)(2,1)} copy(bf16[4,8,2,128,256]{4,3,2,1,0:T(8,128)(2,1)} %bitcast.106) | data formatting | bytes 8388608 | tf_op jit(solution)/shard_map/while/body/eval_jaxpr/gather | solution.py:51
  59.6 4.5 %fusion.56 = (bf16[1,4,8,128,256]{3,2,4,1,0:T(8,128)(2,1)}, bf16[1,4,8,128,256]{3,2,4,1,0:T(8,128)(2,1)}) fusion(bf16[2,4,8,128,256]{3,2,4,1,0:T(8,128)(2,1)} %bitcast.107), kind=kLoop, calls=%fused_computation.106 | loop fusion | bytes 8388608 | tf_op jit(solution)/shard_map/while/body/eval_jaxpr/slice | solution.py:55
  64.1 4.2 %squeeze.19 = bf16[4,1024,4,64]{1,3,2,0:T(8,128)(2,1)} reshape(bf16[1,4,8,128,256]{3,2,4,1,0:T(8,128)(2,1)} %get-tuple-element.30) | data formatting | bytes 4194304 | tf_op jit(solution)/shard_map/while/body/eval_jaxpr/squeeze | solution.py:64
  68.3 4.2 %squeeze.21 = bf16[4,1024,4,64]{1,3,2,0:T(8,128)(2,1)} reshape(bf16[1,4,8,128,256]{3,2,4,1,0:T(8,128)(2,1)} %get-tuple-element.28) | data formatting | bytes 4194304 | tf_op jit(solution)/shard_map/while/body/eval_jaxpr/squeeze | solution.py:55
  72.5 2.9 %fusion = (f32[4,4,128]{2,1,0:T(4,128)S(1)}, f32[4,4,128,1024]{3,2,1,0:T(8,128)S(1)}) fusion(pred[4,1024]{1,0:T(4,128)(4,1)S(1)} %broadcast_compare_fusion, bf16[4,1024,4,64]{1,3,2,0:T(8,128)(2,1)} %squeeze.21, bf16[4,128,4,64]{3,2,1,0:T(4,128)(2,1)S(1)} %reshape.284), kind=kOutput, calls=%fused_computation.5 | convolution fusion | flops 274724864 | bytes 10760192 | tf_op jit(solution)/shard_map/while/body/eval_jaxpr/gqhd,gkhd->ghqk/dot_general | solution.py:54
  75.4 2.1 fusion.1
  77.5 2.2 fusion.39
  80.0 1.5 convolution_convert_fusion.1
  81.5 36.6 %all-reduce.4.cloned.1.call-done = bf16[512,1024]{1,0:T(8,128)(2,1)} async-done(((bf16[512,1024]{1,0:T(8,128)(2,1)}), bf16[512,1024]{1,0:T(8,128)(2,1)}) %all-reduce.4.cloned.1.call-update) | async-done | bytes 1048592 | tf_op jit(solution)/shard_map/psum | solution.py:193
  118.2 1.8 fusion.6
  120.0 1.1 fusion.16
  121.2 0.8 convert_reduce_fusion
  122.0 0.9 fusion.62
  123.0 0.7 fusion.31
  123.7 21.4 %psum.23 = f32[4,128]{1,0:T(4,128)S(1)} all-reduce(f32[4,128]{1,0:T(4,128)S(1)} %get-tuple-element.47), channel_id=1, replica_groups=mesh['nodes'=8,'heads'=4] {'nodes'}, use_global_device_ids=true, to_apply=%region_7.8 | all-reduce | flops 512 | bytes 4096 | tf_op jit(solution)/shard_map/psum | solution.py:151
  145.6 48.5 %all-reduce.6.cloned.1.call-done = f32[4,128,64]{1,2,0:T(8,128)} async-done(((f32[4,128,64]{1,2,0:T(8,128)}), f32[4,128,64]{1,2,0:T(8,128)}) %all-reduce.6.cloned.1.call-update) | async-done | bytes 131088 | tf_op jit(solution)/shard_map/psum | solution.py:151
  194.1 1.6 fusion.21
  195.7 1.5 convolution_convert_fusion
  197.2 0.6 dynamic-slice.2
  198.7 10.4 %all-reduce = s32[32]{0:T(128)S(1)} all-reduce(s32[32]{0:T(128)S(1)} %dynamic-update-slice), channel_id=1, replica_groups=mesh['nodes'=8,'heads'=4] {'nodes'}, use_global_device_ids=true, to_apply=%add | all-reduce | flops 32 | bytes 256
  209.7 0.7 fusion.60
  210.3 1.4 collective-permute-start.7
  211.8 0.7 collective-permute-start.6
  212.4 0.8 collective-permute-start.5
  213.2 1.0 collective-permute-done.7
  214.2 2.2 collective-permute-done.6
  216.4 1.6 collective-permute-done.5
  218.0 2.5 %add_subtract_fusion = s32[4]{0:T(128)S(1)} fusion(s32[1]{0:T(128)} %bitcast.30, s32[1]{0:T(128)} %bitcast.29, s32[1]{0:T(128)} %bitcast.28, s32[1]{0:T(128)} %bitcast.27, s32[]{:T(128)S(6)} %mul.73), kind=kLoop, calls=%fused_computation.102 | loop fusion | flops 16 | bytes 36 | tf_op jit(solution)/shard_map/sub | solution.py:117
  220.6 0.7 reduce-scatter.2.cloned.1.call-done
  221.3 1.1 add_convert_fusion
  222.4 0.6 gather_fusion.1
  223.0 3.4 %collective-permute-start.4 = (bf16[1,1,128,256]{3,2,1,0:T(8,128)(2,1)S(1)}, bf16[1,1,128,256]{3,2,1,0:T(8,128)(2,1)S(1)}, u32[]{:S(2)}, u32[]{:S(2)}) collective-permute-start(bf16[1,1,128,256]{3,2,1,0:T(8,128)(2,1)S(1)} %get-tuple-element.38), channel_id=1, source_target_pairs={{0,24},{4,28},{8,0},{12,4},{16,8},{20,12},{24,16},{28,20},{1,25},{... | collective-permute-start | bytes 196616 | tf_op jit(solution)/shard_map/ppermute | solution.py:17
  226.4 1.1 collective-permute-start.2
  227.5 1.3 collective-permute-done.4
  228.9 3.9 %collective-permute-done.3 = bf16[1,1,128,256]{3,2,1,0:T(8,128)(2,1)S(1)} collective-permute-done((bf16[1,1,128,256]{3,2,1,0:T(8,128)(2,1)S(1)}, bf16[1,1,128,256]{3,2,1,0:T(8,128)(2,1)S(1)}, u32[]{:S(2)}, u32[]{:S(2)}) %collective-permute-start.3) | collective-permute-done | bytes 65568 | tf_op jit(solution)/shard_map/ppermute | solution.py:17
  232.8 1.3 gather_fusion.2
  (62 shorter events, 2.5 us)
Async XLA Ops:
  6.5 23.4 %copy-start = (bf16[3,1024,256]{2,1,0:T(8,128)(2,1)S(1)}, bf16[3,1024,256]{2,1,0:T(8,128)(2,1)}, u32[]{:S(2)}) copy-start(bf16[3,1024,256]{2,1,0:T(8,128)(2,1)} %param.14) | copy-start | bytes 4718596
  6.5 21.9 %all-gather.2.cloned.1.call-start = ((), (), s32[]{:S(2)}) async-start(), calls=%async_computation.1 | async-start | bytes 1310720 | tf_op jit(solution)/shard_map/all_gather | solution.py:182
  7.3 110.9 %all-reduce.4.cloned.1.call-start = ((), (), s32[]{:S(2)}) async-start(), calls=%async_computation.2 | async-start | bytes 2097152 | tf_op jit(solution)/shard_map/psum | solution.py:193
  30.0 8.9 %copy-start.6 = (s32[4]{0:T(128)S(1)}, s32[4]{0:T(128)}, u32[]{:S(2)}) copy-start(s32[4]{0:T(128)} %param.20) | copy-start | bytes 52
  32.3 10.3 %collective-permute-start.1 = (bf16[2,256,256]{2,1,0:T(8,128)(2,1)S(1)}, bf16[2,256,256]{2,1,0:T(8,128)(2,1)S(1)}, u32[]{:S(2)}, u32[]{:S(2)}) collective-permute-start(bf16[2,256,256]{2,1,0:T(8,128)(2,1)S(1)} %get-tuple-element.36), channel_id=1, source_target_pairs={{4,0},{8,4},{12,8},{16,12},{20,16},{24,20},{28,24},{5,1},{9,5},{13... | collective-permute-start | bytes 786440 | tf_op jit(solution)/shard_map/ppermute | solution.py:28
  33.6 14.5 %collective-permute-start = (bf16[2,256,256]{2,1,0:T(8,128)(2,1)S(1)}, bf16[2,256,256]{2,1,0:T(8,128)(2,1)}, u32[]{:S(2)}, u32[]{:S(2)}) collective-permute-start(bf16[2,256,256]{2,1,0:T(8,128)(2,1)S(1)} %get-tuple-element.35), channel_id=1, source_target_pairs={{0,4},{4,8},{8,12},{12,16},{16,20},{20,24},{24,28},{1,5},{5,9},{9,... | collective-permute-start | bytes 786440 | tf_op jit(solution)/shard_map/ppermute | solution.py:27
  75.4 2.1 copy-start.2
  77.5 2.5 %copy-start.4 = (bf16[256,1024]{1,0:T(8,128)(2,1)S(1)}, bf16[256,1024]{1,0:T(8,128)(2,1)}, u32[]{:S(2)}) copy-start(bf16[256,1024]{1,0:T(8,128)(2,1)} %param.15) | copy-start | bytes 1572868
  79.7 38.4 %copy-start.1 = (bf16[512,1024]{1,0:T(8,128)(2,1)S(1)}, bf16[512,1024]{1,0:T(8,128)(2,1)}, u32[]{:S(2)}) copy-start(bf16[512,1024]{1,0:T(8,128)(2,1)} %all-gather.2.cloned.1.call-done) | copy-start | bytes 3145732
  81.5 38.5 %copy-start.9 = (f32[1024]{0:T(1024)S(1)}, f32[1024]{0:T(1024)}, u32[]{:S(2)}) copy-start(f32[1024]{0:T(1024)} %param.16) | copy-start | bytes 12292
  81.5 112.6 %all-reduce.6.cloned.1.call-start = ((), (), s32[]{:S(2)}) async-start(), calls=%async_computation.3 | async-start | bytes 262144 | tf_op jit(solution)/shard_map/psum | solution.py:151
  118.2 1.8 copy-start.7
  119.9 1.2 copy-start.3
  120.0 1.2 copy-start.8
  122.9 98.4 %reduce-scatter.2.cloned.1.call-start = ((), (), s32[]{:S(2)}) async-start(), calls=%async_computation.4 | async-start | bytes 1310720 | tf_op jit(solution)/shard_map/reduce_scatter | solution.py:197
  123.0 72.7 %copy-start.5 = (bf16[256,1024]{1,0:T(8,128)(2,1)S(1)}, bf16[256,1024]{1,0:T(8,128)(2,1)}, u32[]{:S(2)}) copy-start(bf16[256,1024]{1,0:T(8,128)(2,1)} %param.18) | copy-start | bytes 1572868
  194.1 3.2 %copy-start.12 = (u32[32]{0:T(128)S(1)}, u32[32]{0:T(128)}, u32[]{:S(2)}) copy-start(u32[32]{0:T(128)} %constant.121) | copy-start | bytes 388
  194.1 4.4 %copy-start.10 = (s32[4]{0:T(128)S(1)}, s32[4]{0:T(128)}, u32[]{:S(2)}) copy-start(s32[4]{0:T(128)} %param.23) | copy-start | bytes 52
  194.1 15.0 %copy-start.11 = (s32[4]{0:T(128)S(1)}, s32[4]{0:T(128)}, u32[]{:S(2)}) copy-start(s32[4]{0:T(128)} %param.22) | copy-start | bytes 52
  210.3 3.9 %collective-permute-start.7 = (s32[1,1]{1,0:T(1,128)}, s32[1,1]{1,0:T(1,128)}, u32[]{:S(2)}, u32[]{:S(2)}) collective-permute-start(s32[1,1]{1,0:T(1,128)} %get-tuple-element.42), channel_id=1, source_target_pairs={{0,24},{4,28},{8,0},{12,4},{16,8},{20,12},{24,16},{28,20},{1,25},{... | collective-permute-start | bytes 20 | tf_op jit(solution)/shard_map/ppermute | solution.py:17
  211.8 4.6 %collective-permute-start.6 = (s32[1,1]{1,0:T(1,128)}, s32[1,1]{1,0:T(1,128)}, u32[]{:S(2)}, u32[]{:S(2)}) collective-permute-start(s32[1,1]{1,0:T(1,128)} %get-tuple-element.43), channel_id=1, source_target_pairs={{0,16},{4,20},{8,24},{12,28},{16,0},{20,4},{24,8},{28,12},{1,17},{... | collective-permute-start | bytes 20 | tf_op jit(solution)/shard_map/ppermute | solution.py:17
  212.4 5.5 %collective-permute-start.5 = (s32[1,1]{1,0:T(1,128)}, s32[1,1]{1,0:T(1,128)}, u32[]{:S(2)}, u32[]{:S(2)}) collective-permute-start(s32[1,1]{1,0:T(1,128)} %get-tuple-element.44), channel_id=1, source_target_pairs={{0,8},{4,12},{8,16},{12,20},{16,24},{20,28},{24,0},{28,4},{1,9},{5... | collective-permute-start | bytes 20 | tf_op jit(solution)/shard_map/ppermute | solution.py:17
  223.0 5.9 %collective-permute-start.4 = (bf16[1,1,128,256]{3,2,1,0:T(8,128)(2,1)S(1)}, bf16[1,1,128,256]{3,2,1,0:T(8,128)(2,1)S(1)}, u32[]{:S(2)}, u32[]{:S(2)}) collective-permute-start(bf16[1,1,128,256]{3,2,1,0:T(8,128)(2,1)S(1)} %get-tuple-element.38), channel_id=1, source_target_pairs={{0,24},{4,28},{8,0},{12,4},{16,8},{20,12},{24,16},{28,20},{1,25},{... | collective-permute-start | bytes 196616 | tf_op jit(solution)/shard_map/ppermute | solution.py:17
  226.4 6.4 %collective-permute-start.3 = (bf16[1,1,128,256]{3,2,1,0:T(8,128)(2,1)S(1)}, bf16[1,1,128,256]{3,2,1,0:T(8,128)(2,1)S(1)}, u32[]{:S(2)}, u32[]{:S(2)}) collective-permute-start(bf16[1,1,128,256]{3,2,1,0:T(8,128)(2,1)S(1)} %get-tuple-element.39), channel_id=1, source_target_pairs={{0,16},{4,20},{8,24},{12,28},{16,0},{20,4},{24,8},{28,12},{1,17},{... | collective-permute-start | bytes 196616 | tf_op jit(solution)/shard_map/ppermute | solution.py:17
  226.4 6.4 %collective-permute-start.2 = (bf16[1,1,128,256]{3,2,1,0:T(8,128)(2,1)S(1)}, bf16[1,1,128,256]{3,2,1,0:T(8,128)(2,1)S(1)}, u32[]{:S(2)}, u32[]{:S(2)}) collective-permute-start(bf16[1,1,128,256]{3,2,1,0:T(8,128)(2,1)S(1)} %get-tuple-element.40), channel_id=1, source_target_pairs={{0,8},{4,12},{8,16},{12,20},{16,24},{20,28},{24,0},{28,4},{1,9},{5... | collective-permute-start | bytes 196616 | tf_op jit(solution)/shard_map/ppermute | solution.py:17
Sparse Core Ops, SparseCore 0:
  8.9 19.5 all-gather.1
  81.6 36.4 all-reduce.3
  123.0 70.9 all-reduce.5
  197.3 23.9 reduce-scatter.1
where the time goes:
time: 241 us
  waiting for transfers between devices  125 us (52%)
  blocking collectives  31.7 us (13%)
  local copies, waits for them, and re-layouts  28 us (12%)
  matrix products  16 us (7%)
  starting transfers between devices  14.1 us (6%)
  between operations  14.1 us (6%)
  other arithmetic  11.7 us (5%)
    psum x1, waiting for transfers between devices, global_mixing(): summary, key_total = lax.psum((summary, key_total), 'nodes')  48.5 us
    psum x1, waiting for transfers between devices, body(): lax.psum(partial_value.astype(jnp.bfloat16), 'heads').astype(jnp.float32)  36.6 us
    psum x1, blocking collectives, global_mixing(): summary, key_total = lax.psum((summary, key_total), 'nodes')  21.4 us
    all_gather x1, waiting for transfers between devices, body(): full_input = lax.all_gather(nodes_in, 'heads', axis=1, tiled=True)  20.4 us
    unnamed x1, blocking collectives  10.4 us
    gather x2, local copies, waits for them, and re-layouts, one_group(): key_blocks[:, index_group]  10.3 us
    ppermute x6, waiting for transfers between devices, passed_along(): return lax.ppermute(value, axis, pairs)  9.95 us
    ppermute x6, starting transfers between devices, passed_along(): return lax.ppermute(value, axis, pairs)  7.43 us
  transfers between devices with their start and end apart: 12, of which 11 were waited for; matrix products, arithmetic and copies ran while one was open for 3% of the time, Pallas kernels for 0%

commit v1 on v0

v1 whole, which is shorter than its diff:
```python
import functools

import jax
import jax.numpy as jnp
from jax import lax
from jax.experimental import pallas as pl
from jax.experimental.pallas import tpu as pltpu
from jax.sharding import PartitionSpec as P

HD = 64
BLOCK = 128
EPSILON = 1e-06
MESH = pl.DeviceIdType.MESH
BF = jnp.bfloat16
F32 = jnp.float32


def dot(a, b):
    return jnp.dot(a, b, preferred_element_type=F32)


def kernel(
    N, B, SLOTS,
    x_ref, lg_ref, w1_hbm, lo_hbm, gg_ref, w2_hbm, go_hbm, fm_ref, cnt_ref, nb_ref, ids_ref,
    out_ref,
    w1, lo, w2, go, XE, KX, VX, Q, FMB, IDR, LP, LR, LS, LY, HID, PQ, SA, SB, RR, AG,
    QL, HL, GP, GR, GS, GOWN, GY, FB, RB,
    wsem, xcs, xcr, xys, xyr, xfs, xfr, has, har, ids_s, ids_r,
    lcs, lcr, lys, lyr, lhs, lhr, rss, rsr, ags, agr, gcs, gcr, gys, gyr, gzs, gzr,
):
    me = lax.axis_index("nodes")
    h = lax.axis_index("heads")
    y, c = h // 2, h % 2
    pc = h + 1 - 2 * c
    py = h + 2 - 4 * y
    HALF = x_ref.shape[0] // 2
    W = x_ref.shape[1]
    D = 4 * W
    L = 4
    stride = N // L
    NP = W // 128

    def rcopy(src, dst, ss, rs, n, hh):
        return pltpu.make_async_remote_copy(
            src_ref=src, dst_ref=dst, send_sem=ss, recv_sem=rs,
            device_id=(n, hh), device_id_type=MESH)

    weights = [pltpu.make_async_copy(s, d, wsem.at[i])
               for i, (s, d) in enumerate(((w1_hbm, w1), (lo_hbm, lo), (w2_hbm, w2), (go_hbm, go)))]
    for wcopy in weights:
        wcopy.start()

    barrier = pltpu.get_barrier_semaphore()
    for hh in (pc, py):
        pl.semaphore_signal(barrier, inc=1, device_id=(me, hh), device_id_type=MESH)

    @pl.loop(1, N)
    def _(d):
        pl.semaphore_signal(barrier, inc=1, device_id=(lax.rem(me + d, N), h), device_id_type=MESH)

    XE[c, y, 0] = x_ref[0:HALF]
    XE[c, y, 1] = x_ref[HALF:2 * HALF]
    FMB[...] = jnp.zeros_like(FMB)
    for p in range(NP):
        FMB[p, 0:HD, 0:128] = fm_ref[2 * p]
        FMB[p, HD:2 * HD, 128:256] = fm_ref[2 * p + 1]
    IDR[0] = ids_ref[...]

    @pl.when(me == 0)
    def _():
        XE[c, y, 2] = jnp.zeros((HALF, W), BF)

    @pl.when(me == N - 1)
    def _():
        XE[c, y, 3] = jnp.zeros((HALF, W), BF)

    pl.semaphore_wait(barrier, N + 1)

    def piece(k):
        return x_ref.at[pl.ds(k * HALF, HALF)] if k < 2 else XE.at[c, y, k]

    def x_core(k):
        return rcopy(piece(k), XE.at[c, y, k], xcs.at[k], xcr.at[k], me, pc)

    def x_y(k):
        return rcopy(piece(k), XE.at[c, y, k], xys.at[k], xyr.at[k], me, py)

    def x_fwd(k):
        return rcopy(XE.at[c, 1 - y, k], XE.at[c, 1 - y, k], xfs.at[k], xfr.at[k], me, pc)

    up, down = lax.rem(me + 1, N), lax.rem(me + N - 1, N)
    halo_up = rcopy(piece(1), XE.at[c, y, 2], has.at[0], har.at[0], up, h)
    halo_down = rcopy(piece(0), XE.at[c, y, 3], has.at[1], har.at[1], down, h)

    x_y(0).start()
    x_y(1).start()

    @pl.when(me < N - 1)
    def _():
        halo_up.start()

    @pl.when(me > 0)
    def _():
        halo_down.start()

    x_core(0).start()
    x_core(1).start()

    def id_copy(k):
        return rcopy(ids_ref, IDR.at[k], ids_s.at[k], ids_r.at[k], lax.rem(me + k * stride, N), h)

    for k in range(1, L):
        id_copy(k).start()

    x_y(0).wait_recv()
    x_fwd(0).start()

    @pl.when(me > 0)
    def _():
        halo_up.wait_recv()

    x_y(2).start()
    x_core(2).start()
    x_y(1).wait_recv()
    x_fwd(1).start()

    @pl.when(me < N - 1)
    def _():
        halo_down.wait_recv()

    x_y(3).start()
    x_core(3).start()

    def normed(parts, gain_ref):
        floats = [part.astype(F32) for part in parts]
        total = sum(jnp.sum(f * f, axis=-1, keepdims=True) for f in floats)
        scale = lax.rsqrt(total * (1.0 / D) + EPSILON)
        return jnp.concatenate(
            [(f * scale * gain_ref[:, s * W:(s + 1) * W]).astype(BF) for s, f in enumerate(floats)], axis=1)

    def project(k, with_queries):
        x_core(k).wait_recv()
        x_fwd(k).wait_recv()
        rows = normed([XE[s % 2, s // 2, k] for s in range(4)], lg_ref)
        first = (2, 4, 0, 6)[k]
        if with_queries:
            q = (dot(rows, w1[0]).astype(BF).astype(F32) * HD ** (-0.5)).astype(BF)
            Q[2 * k:2 * k + 2] = q.reshape(2, BLOCK, W)
        KX[first:first + 2] = dot(rows, w1[1]).astype(BF).reshape(2, BLOCK, W)
        VX[first:first + 2] = dot(rows, w1[2]).astype(BF).reshape(2, BLOCK, W)

    weights[0].wait()
    project(0, True)
    project(1, True)
    x_y(2).wait_recv()
    x_fwd(2).start()
    x_y(3).wait_recv()
    x_fwd(3).start()
    project(2, False)
    project(3, False)
    weights[1].wait()

    low = lax.broadcasted_iota(jnp.int32, (BLOCK, 128), 1) < HD
    slot_of = lax.broadcasted_iota(jnp.int32, (1, SLOTS * BLOCK), 1) // BLOCK

    def l_core(b):
        return rcopy(LP.at[b, 1 - c], LR.at[b], lcs.at[b], lcr.at[b], me, pc)

    def l_y(b):
        return rcopy(LS.at[b], LY.at[b], lys.at[b], lyr.at[b], me, py)

    def l_hid(b):
        return rcopy(HID.at[b, c], HID.at[b, c], lhs.at[b], lhr.at[b], me, pc)

    def l_reduce(b):
        l_core(b).wait_recv()
        LS[b] = (LP[b, c].astype(F32) + LR[b].astype(F32)).astype(BF)
        l_y(b).start()

    @pl.loop(0, B)
    def _(b):
        picks = [jnp.clip(nb_ref[b, s] - (me * B - 2), 0, 2 * B - 1) for s in range(SLOTS)]
        live = slot_of < cnt_ref[b]
        mixed = []
        for p in range(NP):
            cols = slice(p * 128, (p + 1) * 128)
            q = Q[b, :, cols].astype(F32)
            both = jnp.concatenate([jnp.where(low, q, 0.0), jnp.where(low, 0.0, q)], axis=0).astype(BF)
            keys = jnp.concatenate([KX[i, :, cols] for i in picks], axis=0)
            vals = jnp.concatenate([VX[i, :, cols] for i in picks], axis=0)
            scores = lax.dot_general(both, keys, (((1,), (1,)), ((), ())), preferred_element_type=F32)
            scores = jnp.where(live, scores, -1e30)
            expo = jnp.exp(scores - jnp.max(scores, axis=-1, keepdims=True))
            totals = jnp.sum(expo, axis=-1, keepdims=True)
            o = dot(expo.astype(BF), vals) / totals
            mixed.append(jnp.where(low, o[:BLOCK], o[BLOCK:]).astype(BF))
        part = dot(jnp.concatenate(mixed, axis=1), lo[...]).astype(BF)
        for s in range(4):
            LP[b, s % 2, s // 2] = part[:, s * W:(s + 1) * W]
        l_core(b).start()

        @pl.when(b > 0)
        def _():
            l_reduce(b - 1)

    l_reduce(B - 1)
    weights[2].wait()
    SA[...] = jnp.zeros_like(SA)

    def features(rows, p):
        u = dot(rows[:, p * 128:(p + 1) * 128], FMB[p]) * HD ** (-0.5)
        return jnp.where(u > 0, u + 1.0, jnp.exp(jnp.minimum(u, 0.0))).astype(BF)

    def global_block(b):
        l_hid(b).wait_recv()
        rows = normed([HID[b, s % 2, s // 2] for s in range(4)], gg_ref)
        gq = dot(rows, w2[0]).astype(BF)
        gk = dot(rows, w2[1]).astype(BF)
        gv = dot(rows, w2[2]).astype(BF).astype(F32)
        for p in range(NP):
            PQ[b, :, p * 256:(p + 1) * 256] = features(gq, p)
            fk = features(gk, p)
            v = gv[:, p * 128:(p + 1) * 128]
            for side in range(2):
                ext = (jnp.where(low, v, 1.0) if side == 0 else jnp.where(low, 1.0, v)).astype(BF)
                head = 2 * p + side
                SA[head * 128:(head + 1) * 128] += lax.dot_general(
                    fk[:, side * 128:(side + 1) * 128], ext, (((0,), (0,)), ((), ())),
                    preferred_element_type=F32)

    @pl.loop(0, B)
    def _(b):
        l_y(b).wait_recv()
        for yy in range(2):
            own = XE[c, yy, b // 2, pl.ds(pl.multiple_of((b % 2) * BLOCK, BLOCK), BLOCK)].astype(F32)
            HID[b, c, yy] = (own + (LS[b, yy].astype(F32) + LY[b, yy].astype(F32))).astype(BF)
        l_hid(b).start()

        @pl.when(b > 0)
        def _():
            global_block(b - 1)

    global_block(B - 1)

    SB[...] = SA[...].reshape(SB.shape).astype(BF)

    def rs_copy(d):
        to = lax.rem(me + d, N)
        return rcopy(SB.at[to], RR.at[d], rss.at[d], rsr.at[d], to, h)

    def ag_copy(d):
        to = lax.rem(me + d, N)
        return rcopy(AG.at[me], AG.at[me], ags.at[d], agr.at[d], to, h)

    def ag_arrival(d):
        origin = lax.rem(me + N - d, N)
        return rcopy(AG.at[origin], AG.at[origin], ags.at[d], agr.at[d], lax.rem(me + d, N), h)

    @pl.loop(1, N)
    def _(d):
        rs_copy(d).start()

    for k in range(1, L):
        id_copy(k).wait_recv()

    def weight(id_row, rows):
        same = jnp.zeros((1, 128), F32)
        for j in range(B):
            same = same + jnp.where(id_row == rows[j:j + 1], 1.0, 0.0)
        return same

    def wide(w, width):
        return jnp.concatenate([w] * (width // 128), axis=1)

    for k in range(L):
        hashed = IDR[(L - k) % L][B:2 * B]
        q_sum, h_sum = None, None
        for i in range(B):
            w = weight(ids_ref[i:i + 1], hashed)
            qt = wide(w, 2 * W) * PQ[i].astype(F32)
            ht = wide(w, W) * HID[i, c, y].astype(F32)
            q_sum = qt if q_sum is None else q_sum + qt
            h_sum = ht if h_sum is None else h_sum + ht
        QL[k] = q_sum.astype(BF)
        HL[k] = h_sum

    RR[0] = SB[me]

    @pl.loop(1, N)
    def _(d):
        rs_copy(d).wait_recv()

    AG[me] = jnp.sum(RR[...].astype(F32), axis=0).astype(BF)

    @pl.loop(1, N)
    def _(d):
        ag_copy(d).start()

    weights[3].wait()

    @pl.loop(1, N)
    def _(d):
        ag_arrival(d).wait_recv()

    SA[...] = AG[...].astype(F32).reshape(SA.shape)

    def g_core(k):
        return rcopy(GP.at[k, 1 - c], GR.at[k], gcs.at[k], gcr.at[k], me, pc)

    def g_y(k):
        return rcopy(GS.at[k], GY.at[k], gys.at[k], gyr.at[k], me, py)

    def g_z(k):
        return rcopy(FB.at[k], RB.at[k], gzs.at[k], gzr.at[k], lax.rem(me + k * stride, N), h)

    def mix(k):
        mixed = []
        for p in range(NP):
            r = []
            for side in range(2):
                head = 2 * p + side
                r.append(dot(QL[k, :, head * 128:(head + 1) * 128],
                             SA[head * 128:(head + 1) * 128].astype(BF)))
            top = jnp.where(low, r[0], r[1])
            below = pltpu.roll(jnp.where(low, r[1], r[0]), HD, 1)
            mixed.append((top / below).astype(BF))
        part = dot(jnp.concatenate(mixed, axis=1), go[...]).astype(BF)
        for s in range(4):
            GP[k, s % 2, s // 2] = part[:, s * W:(s + 1) * W]
        g_core(k).start()

    def g_reduce(k):
        g_core(k).wait_recv()
        GS[k] = (GP[k, c, 1 - y].astype(F32) + GR[k, 1 - y].astype(F32)).astype(BF)
        g_y(k).start()
        GOWN[k] = GP[k, c, y].astype(F32) + GR[k, y].astype(F32)

    order = (2, 1, 3, 0)
    for t, k in enumerate(order):
        mix(k)
        if t > 0:
            g_reduce(order[t - 1])
    g_reduce(order[-1])
    for k in order:
        g_y(k).wait_recv()
        final = (HL[k] + (GOWN[k] + GY[k].astype(F32))).astype(BF)
        if k:
            FB[k] = final
            g_z(k).start()
        else:
            RB[0] = final
    for k in range(1, L):
        g_z(k).wait_recv()
    for j in range(B):
        acc = None
        for k in range(L):
            w = weight(ids_ref[B + j:B + j + 1], IDR[k][0:B])
            term = wide(w, W) * RB[k].astype(F32)
            acc = term if acc is None else acc + term
        out_ref[j * BLOCK:(j + 1) * BLOCK] = acc.astype(BF)

    for k in range(4):
        x_y(k).wait_send()
        x_core(k).wait_send()
        x_fwd(k).wait_send()

    @pl.when(me < N - 1)
    def _():
        halo_up.wait_send()

    @pl.when(me > 0)
    def _():
        halo_down.wait_send()

    for k in range(1, L):
        id_copy(k).wait_send()
        g_z(k).wait_send()
    for b in range(B):
        l_core(b).wait_send()
        l_y(b).wait_send()
        l_hid(b).wait_send()
        g_core(b).wait_send()
        g_y(b).wait_send()

    @pl.loop(1, N)
    def _(d):
        rs_copy(d).wait_send()
        ag_copy(d).wait_send()


def body(
    N, nodes_in, local_gain, w1, local_out, global_gain, w2, global_out, feature_map,
    neighbour_count, neighbour_blocks, metis_order, hashed_order,
):
    rows, W = nodes_in.shape
    B = metis_order.shape[0]
    SLOTS = neighbour_blocks.shape[1]
    D = w1.shape[1]
    SR = feature_map.shape[0] * feature_map.shape[2]
    ids = jnp.concatenate([metis_order, hashed_order])
    ids = jnp.broadcast_to(ids[:, None], (2 * B, 128))
    vm = pl.BlockSpec(memory_space=pltpu.VMEM)
    sm = pl.BlockSpec(memory_space=pltpu.SMEM)
    hb = pl.BlockSpec(memory_space=pl.ANY)

    def V(*shape, dtype=BF):
        return pltpu.VMEM(shape, dtype)

    half = rows // 2
    S = pltpu.SemaphoreType.DMA
    scratch = [
        V(3, D, W), V(W, D), V(3, D, W), V(W, D),
        V(2, 2, 4, half, W), V(2 * B, BLOCK, W), V(2 * B, BLOCK, W), V(B, BLOCK, W),
        V(W // 128, 128, 256), V(4, 2 * B, 128, dtype=jnp.int32),
        V(B, 2, 2, BLOCK, W), V(B, 2, BLOCK, W), V(B, 2, BLOCK, W), V(B, 2, BLOCK, W),
        V(B, 2, 2, BLOCK, W), V(B, BLOCK, 2 * W), V(SR, 128, dtype=F32),
        V(N, SR // N, 128), V(N, SR // N, 128), V(N, SR // N, 128),
        V(4, BLOCK, 2 * W), V(4, BLOCK, W, dtype=F32),
        V(4, 2, 2, BLOCK, W), V(4, 2, BLOCK, W), V(4, BLOCK, W), V(4, BLOCK, W, dtype=F32),
        V(4, BLOCK, W), V(4, BLOCK, W), V(4, BLOCK, W),
        S((4,)),
    ] + [S((4,))] * 6 + [S((2,))] * 2 + [S((4,))] * 2 + [S((4,))] * 6 + [S((N,))] * 4 + [S((4,))] * 6
    return pl.pallas_call(
        functools.partial(kernel, N, B, SLOTS),
        out_shape=jax.ShapeDtypeStruct((rows, W), BF),
        in_specs=[vm, vm, hb, hb, vm, hb, hb, vm, sm, sm, vm],
        out_specs=vm,
        scratch_shapes=scratch,
        compiler_params=pltpu.CompilerParams(
            collective_id=0, has_side_effects=True, vmem_limit_bytes=48 * 1024 * 1024),
        name="graph_pair",
    )(nodes_in, local_gain.reshape(1, D), w1, local_out, global_gain.reshape(1, D), w2, global_out,
      feature_map, neighbour_count, neighbour_blocks, ids)


def solution(mesh):
    in_specs = (
        P("nodes", "heads"), P(), P(None, None, "heads"), P("heads", None), P(),
        P(None, None, "heads"), P("heads", None), P("heads", None, None),
        P("nodes"), P("nodes", None), P("nodes"), P("nodes"),
    )
    return jax.shard_map(
        functools.partial(body, mesh.shape["nodes"]), mesh=mesh, in_specs=in_specs,
        out_specs=P("nodes", "heads"), check_vma=False)
```

time: 241 us -> 76.3 us (0.32)
  waiting for transfers between devices: 125 us -> 0 us
  Pallas kernels: 0 us -> 64.9 us
  blocking collectives: 31.7 us -> 0 us
  local copies, waits for them, and re-layouts: 28 us -> 10.2 us
  matrix products: 16 us -> 0 us
  starting transfers between devices: 14.1 us -> 0 us
  between operations: 14.1 us -> 0.02 us
  other arithmetic: 11.7 us -> 0.75 us
    psum x2 -> x0, waiting for transfers between devices: 85.1 us -> none  [the longest x1 48.5 us: global_mixing(): summary, key_total = lax.psum((summary, key_total), 'nodes')]
    pallas_call x0 -> x1, Pallas kernels: none -> 64.9 us  [body(): pl.pallas_call(functools.partial(kernel, N, B, SLOTS), out_shape=jax.Shap...]
    psum x1 -> x0, blocking collectives: 21.4 us -> none  [global_mixing(): summary, key_total = lax.psum((summary, key_total), 'nodes')]
    all_gather x1 -> x0, waiting for transfers between devices: 20.4 us -> none  [body(): full_input = lax.all_gather(nodes_in, 'heads', axis=1, tiled=True)]
    ppermute x8 -> x0, waiting for transfers between devices: 18.1 us -> none  [the longest x6 9.95 us: passed_along(): return lax.ppermute(value, axis, pairs)]
    dot_general x11 -> x0, matrix products: 16 us -> none  [the longest x1 2.91 us: one_group(): jnp.einsum('gqhd,gkhd->ghqk', query_group, picked[0], preferred_element_t...]
    ppermute x8 -> x0, starting transfers between devices: 14 us -> none  [the longest x6 7.43 us: passed_along(): return lax.ppermute(value, axis, pairs)]
    gather x4 -> x0, local copies, waits for them, and re-layouts: 12.1 us -> none  [the longest x2 10.3 us: one_group(): key_blocks[:, index_group]]
  transfers between devices with their start and end apart: 12 -> 0, of which waited for: 11 -> 0; matrix products, arithmetic and copies ran while one was open for 3% -> 0% of each run, Pallas kernels for 0% -> 0%
where the time goes in v1:
time: 76.3 us; the launch traced here: 75.8 us
  Pallas kernels  64.9 us (85%)
  local copies, waits for them, and re-layouts  10.2 us (13%)
    pallas_call x1, Pallas kernels, body(): pl.pallas_call(functools.partial(kernel, N, B, SLOTS), out_shape=jax.Shap...  64.9 us
    unnamed x21, local copies, waits for them, and re-layouts  10.1 us

profile of v1, /device:TPU:0, one launch (start us, length us, event | category | flops | bytes accessed | tf_op | source)
XLA Modules:
  0.0 75.8 jit_solution(10875063377864216206)
XLA Ops:
  0.0 0.7 pad_add_fusion
  0.7 0.1 broadcast_in_dim.2.ids_ref
  0.8 0.0 copy-start
  0.8 1.4 %copy-done = bf16[3,1024,256]{2,1,0:T(8,128)(2,1)S(1)} copy-done((bf16[3,1024,256]{2,1,0:T(8,128)(2,1)S(1)}, bf16[3,1024,256]{2,1,0:T(8,128)(2,1)}, u32[]{:S(2)}) %copy-start) | copy-done | bytes 1572888
  2.2 0.0 copy-start.1
  2.2 1.4 %copy-done.1 = bf16[3,1024,256]{2,1,0:T(8,128)(2,1)S(1)} copy-done((bf16[3,1024,256]{2,1,0:T(8,128)(2,1)S(1)}, bf16[3,1024,256]{2,1,0:T(8,128)(2,1)}, u32[]{:S(2)}) %copy-start.1) | copy-done | bytes 1572888
  3.6 0.0 copy-start.2
  3.6 1.0 %copy-done.2 = bf16[256,1024]{1,0:T(8,128)(2,1)S(1)} copy-done((bf16[256,1024]{1,0:T(8,128)(2,1)S(1)}, bf16[256,1024]{1,0:T(8,128)(2,1)}, u32[]{:S(2)}) %copy-start.2) | copy-done | bytes 524312
  4.7 0.0 copy-start.3
  4.7 1.0 %copy-done.3 = bf16[256,1024]{1,0:T(8,128)(2,1)S(1)} copy-done((bf16[256,1024]{1,0:T(8,128)(2,1)S(1)}, bf16[256,1024]{1,0:T(8,128)(2,1)}, u32[]{:S(2)}) %copy-start.3) | copy-done | bytes 524312
  5.7 0.0 copy-start.4
  5.7 0.9 %copy-done.4 = bf16[512,256]{1,0:T(8,128)(2,1)S(1)} copy-done((bf16[512,256]{1,0:T(8,128)(2,1)S(1)}, bf16[512,256]{1,0:T(8,128)(2,1)}, u32[]{:S(2)}) %copy-start.4) | copy-done | bytes 262168
  6.7 0.0 copy-start.5
  6.7 0.8 %copy-done.5 = bf16[4,64,128]{2,1,0:T(8,128)(2,1)S(1)} copy-done((bf16[4,64,128]{2,1,0:T(8,128)(2,1)S(1)}, bf16[4,64,128]{2,1,0:T(8,128)(2,1)}, u32[]{:S(2)}) %copy-start.5) | copy-done | bytes 65560
  7.5 0.0 copy-start.6
  7.5 0.7 copy-done.6
  8.2 0.0 copy-start.7
  8.2 0.7 copy-done.7
  8.9 0.0 copy-start.8
  8.9 0.7 copy-done.8
  9.6 0.0 copy-start.9
  9.6 0.7 copy-done.9
  10.2 64.9 %graph_pair.1 = bf16[512,256]{1,0:T(8,128)(2,1)S(1)} custom-call(bf16[512,256]{1,0:T(8,128)(2,1)S(1)} %copy-done.4, f32[1,1024]{1,0:T(1,128)S(1)} %bitcast.2, bf16[3,1024,256]{2,1,0:T(8,128)(2,1)S(1)} %copy-done, bf16[256,1024]{1,0:T(8,128)(2,1)S(1)} %copy-done.2, f32[1,1024]{1,0:T(1,128)S(1)} %bitcast.3, bf16[3,1024,256]{2,1,0:T(8,128)(2,1)S(1)} %copy-done.1, ...), custom_call_target="tpu_custom_call" | custom-call | tf_op jit(solution)/shard_map/graph_pair/pallas_call | solution.py:423
  75.1 0.7 copy.14
Async XLA Ops:
  0.8 1.4 %copy-start = (bf16[3,1024,256]{2,1,0:T(8,128)(2,1)S(1)}, bf16[3,1024,256]{2,1,0:T(8,128)(2,1)}, u32[]{:S(2)}) copy-start(bf16[3,1024,256]{2,1,0:T(8,128)(2,1)} %w1_hbm.1) | copy-start | bytes 4718596
  2.2 1.4 %copy-start.1 = (bf16[3,1024,256]{2,1,0:T(8,128)(2,1)S(1)}, bf16[3,1024,256]{2,1,0:T(8,128)(2,1)}, u32[]{:S(2)}) copy-start(bf16[3,1024,256]{2,1,0:T(8,128)(2,1)} %w2_hbm.1) | copy-start | bytes 4718596
  3.6 1.0 %copy-start.2 = (bf16[256,1024]{1,0:T(8,128)(2,1)S(1)}, bf16[256,1024]{1,0:T(8,128)(2,1)}, u32[]{:S(2)}) copy-start(bf16[256,1024]{1,0:T(8,128)(2,1)} %lo_hbm.1) | copy-start | bytes 1572868
  4.7 1.0 %copy-start.3 = (bf16[256,1024]{1,0:T(8,128)(2,1)S(1)}, bf16[256,1024]{1,0:T(8,128)(2,1)}, u32[]{:S(2)}) copy-start(bf16[256,1024]{1,0:T(8,128)(2,1)} %go_hbm.1) | copy-start | bytes 1572868
  5.7 0.9 %copy-start.4 = (bf16[512,256]{1,0:T(8,128)(2,1)S(1)}, bf16[512,256]{1,0:T(8,128)(2,1)}, u32[]{:S(2)}) copy-start(bf16[512,256]{1,0:T(8,128)(2,1)} %x_ref.1) | copy-start | bytes 786436
  6.7 0.8 %copy-start.5 = (bf16[4,64,128]{2,1,0:T(8,128)(2,1)S(1)}, bf16[4,64,128]{2,1,0:T(8,128)(2,1)}, u32[]{:S(2)}) copy-start(bf16[4,64,128]{2,1,0:T(8,128)(2,1)} %fm_ref.1) | copy-start | bytes 196612
  7.5 0.7 copy-start.6
  8.2 0.7 copy-start.7
  8.9 0.7 copy-start.8
  9.6 0.7 copy-start.9

commit v2 on v1

--- a/solution.py
+++ b/solution.py
@@ -21,11 +21,11 @@
 
 def kernel(
     N, B, SLOTS,
-    x_ref, lg_ref, w1_hbm, lo_hbm, gg_ref, w2_hbm, go_hbm, fm_ref, cnt_ref, nb_ref, ids_ref,
+    x_hbm, lg_hbm, w1_hbm, lo_hbm, gg_hbm, w2_hbm, go_hbm, fm_hbm, cnt_hbm, nb_hbm, metis_hbm, hashed_hbm,
     out_ref,
-    w1, lo, w2, go, XE, KX, VX, Q, FMB, IDR, LP, LR, LS, LY, HID, PQ, SA, SB, RR, AG,
+    x_ref, lg_ref, gg_ref, fm_ref, cnt_ref, nb_ref, metis_ref, hashed_ref, ids_ref, OF, w1, lo, w2, go, XE, KX, VX, Q, FMB, IDR, LP, LR, LS, LY, HID, PQ, SA, SB, RR, AG,
     QL, HL, GP, GR, GS, GOWN, GY, FB, RB,
-    wsem, xcs, xcr, xys, xyr, xfs, xfr, has, har, ids_s, ids_r,
+    isem, wsem, xcs, xcr, xys, xyr, xfs, xfr, has, har, ids_s, ids_r,
     lcs, lcr, lys, lyr, lhs, lhr, rss, rsr, ags, agr, gcs, gcr, gys, gyr, gzs, gzr,
 ):
     me = lax.axis_index("nodes")
@@ -45,25 +45,34 @@
             src_ref=src, dst_ref=dst, send_sem=ss, recv_sem=rs,
             device_id=(n, hh), device_id_type=MESH)
 
+    barrier = pltpu.get_barrier_semaphore()
+
+    @pl.loop(1, N)
+    def _(d):
+        pl.semaphore_signal(barrier, inc=1, device_id=(lax.rem(me + d, N), h), device_id_type=MESH)
+
+    for hh in (pc, py):
+        pl.semaphore_signal(barrier, inc=1, device_id=(me, hh), device_id_type=MESH)
+
+    small = [pltpu.make_async_copy(s, d, isem.at[i])
+             for i, (s, d) in enumerate((
+                 (x_hbm, x_ref), (metis_hbm, metis_ref), (hashed_hbm, hashed_ref), (fm_hbm, fm_ref),
+                 (lg_hbm, lg_ref), (gg_hbm, gg_ref), (cnt_hbm, cnt_ref), (nb_hbm, nb_ref)))]
     weights = [pltpu.make_async_copy(s, d, wsem.at[i])
                for i, (s, d) in enumerate(((w1_hbm, w1), (lo_hbm, lo), (w2_hbm, w2), (go_hbm, go)))]
-    for wcopy in weights:
-        wcopy.start()
-
-    barrier = pltpu.get_barrier_semaphore()
-    for hh in (pc, py):
-        pl.semaphore_signal(barrier, inc=1, device_id=(me, hh), device_id_type=MESH)
-
-    @pl.loop(1, N)
-    def _(d):
-        pl.semaphore_signal(barrier, inc=1, device_id=(lax.rem(me + d, N), h), device_id_type=MESH)
-
+    for each in small + weights:
+        each.start()
+    FMB[...] = jnp.zeros_like(FMB)
+    for each in small:
+        each.wait()
     XE[c, y, 0] = x_ref[0:HALF]
     XE[c, y, 1] = x_ref[HALF:2 * HALF]
-    FMB[...] = jnp.zeros_like(FMB)
     for p in range(NP):
         FMB[p, 0:HD, 0:128] = fm_ref[2 * p]
         FMB[p, HD:2 * HD, 128:256] = fm_ref[2 * p + 1]
+    for j in range(B):
+        ids_ref[j:j + 1] = jnp.full((1, 128), metis_ref[j], jnp.int32)
+        ids_ref[B + j:B + j + 1] = jnp.full((1, 128), hashed_ref[j], jnp.int32)
     IDR[0] = ids_ref[...]
 
     @pl.when(me == 0)
@@ -72,7 +81,8 @@
 
     @pl.when(me == N - 1)
     def _():
-        XE[c, y, 3] = jnp.zeros((HALF, W), BF)
+        XE[c, 0, 3] = jnp.zeros((HALF, W), BF)
+        XE[c, 1, 3] = jnp.zeros((HALF, W), BF)
 
     pl.semaphore_wait(barrier, N + 1)
 
@@ -92,6 +102,8 @@
     halo_up = rcopy(piece(1), XE.at[c, y, 2], has.at[0], har.at[0], up, h)
     halo_down = rcopy(piece(0), XE.at[c, y, 3], has.at[1], har.at[1], down, h)
 
+    halo_far = rcopy(XE.at[c, 1 - y, 0], XE.at[c, 1 - y, 3], has.at[2], har.at[2], down, h)
+
     x_y(0).start()
     x_y(1).start()
 
@@ -114,6 +126,10 @@
 
     x_y(0).wait_recv()
     x_fwd(0).start()
+
+    @pl.when(me > 0)
+    def _():
+        halo_far.start()
 
     @pl.when(me > 0)
     def _():
@@ -128,7 +144,6 @@
     def _():
         halo_down.wait_recv()
 
-    x_y(3).start()
     x_core(3).start()
 
     def normed(parts, gain_ref):
@@ -154,7 +169,11 @@
     project(1, True)
     x_y(2).wait_recv()
     x_fwd(2).start()
-    x_y(3).wait_recv()
+
+    @pl.when(me < N - 1)
+    def _():
+        halo_far.wait_recv()
+
     x_fwd(3).start()
     project(2, False)
     project(3, False)
@@ -211,14 +230,17 @@
         u = dot(rows[:, p * 128:(p + 1) * 128], FMB[p]) * HD ** (-0.5)
         return jnp.where(u > 0, u + 1.0, jnp.exp(jnp.minimum(u, 0.0))).astype(BF)
 
+    def global_queries(b, rows):
+        gq = dot(rows, w2[0]).astype(BF)
+        for p in range(NP):
+            PQ[b, :, p * 256:(p + 1) * 256] = features(gq, p)
+
     def global_block(b):
         l_hid(b).wait_recv()
         rows = normed([HID[b, s % 2, s // 2] for s in range(4)], gg_ref)
-        gq = dot(rows, w2[0]).astype(BF)
         gk = dot(rows, w2[1]).astype(BF)
         gv = dot(rows, w2[2]).astype(BF).astype(F32)
         for p in range(NP):
-            PQ[b, :, p * 256:(p + 1) * 256] = features(gq, p)
             fk = features(gk, p)
             v = gv[:, p * 128:(p + 1) * 128]
             for side in range(2):
@@ -227,6 +249,7 @@
                 SA[head * 128:(head + 1) * 128] += lax.dot_general(
                     fk[:, side * 128:(side + 1) * 128], ext, (((0,), (0,)), ((), ())),
                     preferred_element_type=F32)
+        return rows
 
     @pl.loop(0, B)
     def _(b):
@@ -238,9 +261,9 @@
 
         @pl.when(b > 0)
         def _():
-            global_block(b - 1)
-
-    global_block(B - 1)
+            global_queries(b - 1, global_block(b - 1))
+
+    last_rows = global_block(B - 1)
 
     SB[...] = SA[...].reshape(SB.shape).astype(BF)
 
@@ -260,6 +283,7 @@
     def _(d):
         rs_copy(d).start()
 
+    global_queries(B - 1, last_rows)
     for k in range(1, L):
         id_copy(k).wait_recv()
 
@@ -349,18 +373,24 @@
             g_z(k).start()
         else:
             RB[0] = final
-    for k in range(1, L):
+
+    def placed(k, j):
+        w = weight(ids_ref[B + j:B + j + 1], IDR[k][0:B])
+        return wide(w, W) * RB[k].astype(F32)
+
+    for j in range(B):
+        OF[j] = placed(0, j)
+    for k in order[:-2]:
         g_z(k).wait_recv()
+        for j in range(B):
+            OF[j] += placed(k, j)
+    g_z(order[-2]).wait_recv()
     for j in range(B):
-        acc = None
-        for k in range(L):
-            w = weight(ids_ref[B + j:B + j + 1], IDR[k][0:B])
-            term = wide(w, W) * RB[k].astype(F32)
-            acc = term if acc is None else acc + term
-        out_ref[j * BLOCK:(j + 1) * BLOCK] = acc.astype(BF)
-
+        out_ref[j * BLOCK:(j + 1) * BLOCK] = (OF[j] + placed(order[-2], j)).astype(BF)
+
+    for k in range(3):
+        x_y(k).wait_send()
     for k in range(4):
-        x_y(k).wait_send()
         x_core(k).wait_send()
         x_fwd(k).wait_send()
 
@@ -371,6 +401,7 @@
     @pl.when(me > 0)
     def _():
         halo_down.wait_send()
+        halo_far.wait_send()
 
     for k in range(1, L):
         id_copy(k).wait_send()
@@ -397,10 +428,7 @@
     SLOTS = neighbour_blocks.shape[1]
     D = w1.shape[1]
     SR = feature_map.shape[0] * feature_map.shape[2]
-    ids = jnp.concatenate([metis_order, hashed_order])
-    ids = jnp.broadcast_to(ids[:, None], (2 * B, 128))
     vm = pl.BlockSpec(memory_space=pltpu.VMEM)
-    sm = pl.BlockSpec(memory_space=pltpu.SMEM)
     hb = pl.BlockSpec(memory_space=pl.ANY)
 
     def V(*shape, dtype=BF):
@@ -409,6 +437,10 @@
     half = rows // 2
     S = pltpu.SemaphoreType.DMA
     scratch = [
+        V(rows, W), V(1, D, dtype=F32), V(1, D, dtype=F32), V(*feature_map.shape),
+        pltpu.SMEM((B,), jnp.int32), pltpu.SMEM((B, SLOTS), jnp.int32),
+        pltpu.SMEM((B,), jnp.int32), pltpu.SMEM((B,), jnp.int32),
+        V(2 * B, 128, dtype=jnp.int32), V(B, BLOCK, W, dtype=F32),
         V(3, D, W), V(W, D), V(3, D, W), V(W, D),
         V(2, 2, 4, half, W), V(2 * B, BLOCK, W), V(2 * B, BLOCK, W), V(B, BLOCK, W),
         V(W // 128, 128, 256), V(4, 2 * B, 128, dtype=jnp.int32),
@@ -418,19 +450,19 @@
         V(4, BLOCK, 2 * W), V(4, BLOCK, W, dtype=F32),
         V(4, 2, 2, BLOCK, W), V(4, 2, BLOCK, W), V(4, BLOCK, W), V(4, BLOCK, W, dtype=F32),
         V(4, BLOCK, W), V(4, BLOCK, W), V(4, BLOCK, W),
-        S((4,)),
-    ] + [S((4,))] * 6 + [S((2,))] * 2 + [S((4,))] * 2 + [S((4,))] * 6 + [S((N,))] * 4 + [S((4,))] * 6
+        S((8,)), S((4,)),
+    ] + [S((4,))] * 6 + [S((3,))] * 2 + [S((4,))] * 2 + [S((4,))] * 6 + [S((N,))] * 4 + [S((4,))] * 6
     return pl.pallas_call(
         functools.partial(kernel, N, B, SLOTS),
         out_shape=jax.ShapeDtypeStruct((rows, W), BF),
-        in_specs=[vm, vm, hb, hb, vm, hb, hb, vm, sm, sm, vm],
+        in_specs=[hb] * 12,
         out_specs=vm,
         scratch_shapes=scratch,
         compiler_params=pltpu.CompilerParams(
-            collective_id=0, has_side_effects=True, vmem_limit_bytes=48 * 1024 * 1024),
+            collective_id=0, has_side_effects=True, vmem_limit_bytes=67043328),
         name="graph_pair",
     )(nodes_in, local_gain.reshape(1, D), w1, local_out, global_gain.reshape(1, D), w2, global_out,
-      feature_map, neighbour_count, neighbour_blocks, ids)
+      feature_map, neighbour_count, neighbour_blocks, metis_order, hashed_order)
 
 
 def solution(mesh):

time: 76.3 us -> 67.1 us (0.88)
  local copies, waits for them, and re-layouts: 10.2 us -> 1.67 us
    unnamed x21 -> x1, local copies, waits for them, and re-layouts: 10.1 us -> 1.67 us
where the time goes in v2:
time: 67.1 us; the launch traced here: 66.9 us
  Pallas kernels  65.2 us (97%)
  local copies, waits for them, and re-layouts  1.67 us (2%)
    pallas_call x1, Pallas kernels, body(): pl.pallas_call(functools.partial(kernel, N, B, SLOTS), out_shape=jax.Shap...  65.2 us
    unnamed x1, local copies, waits for them, and re-layouts  1.67 us

profile of v2, /device:TPU:0, one launch (start us, length us, event | category | flops | bytes accessed | tf_op | source)
XLA Modules:
  0.0 66.9 jit_solution(227469882807181396)
XLA Ops:
  0.0 65.2 %graph_pair.1 = bf16[512,256]{1,0:T(8,128)(2,1)} custom-call(bf16[512,256]{1,0:T(8,128)(2,1)} %x_hbm.1, f32[1,1024]{1,0:T(1,128)} %bitcast.2, bf16[3,1024,256]{2,1,0:T(8,128)(2,1)} %w1_hbm.1, bf16[256,1024]{1,0:T(8,128)(2,1)} %lo_hbm.1, f32[1,1024]{1,0:T(1,128)} %bitcast.3, bf16[3,1024,256]{2,1,0:T(8,128)(2,1)} %w2_hbm.1, bf16[256,1024]{1,0:T(8,128)(2,1)} %go_hbm.1, ...), custom_call_target="tpu_custom_call" | custom-call | tf_op jit(solution)/shard_map/graph_pair/pallas_call | solution.py:455
  65.2 1.7 %copy.14 = bf16[512,256]{1,0:T(8,128)(2,1)} copy(bf16[512,256]{1,0:T(8,128)(2,1)} %graph_pair.1) | data formatting | bytes 524288
